TPU v7x, 256 devices: a whole 4x4x8 slice. The times are simulated.
256 devices in a mesh: view: 8 (over x, core), gauss: 32 (over y, z).
Axes of the slice: x: 4, y: 4, z: 8, core: 2. Of those that a mesh axis runs over, the one named last changes fastest.
Arguments:
- means: float32 [3, 524288], P(None, 'gauss'), may hold values from -1 to 1
- scales: float32 [3, 524288], P(None, 'gauss'), may hold values from 0.05 to 0.6
- quats: float32 [4, 524288], P(None, 'gauss'), may hold values from -6 to 6
- attrs: float32 [49, 524288], P(None, 'gauss'), may hold values from -6 to 6
- grad_screen: float32 [32, 2, 524288], P('view', None, 'gauss'), may hold values from -6 to 6
- visible: int32 [32, 524288], P('view', 'gauss'), may hold values 0 or 1
- clone_mask: int32 [524288], P('gauss'), may hold values from 0 to 1, as said below
- rotation: float32 [32, 3, 3], P('view'), may hold values from -3.5 to 3.5
- shift: float32 [32, 3], P('view'), may hold values from 2 to 5
- focal: float32 [32], P('view'), may hold values from 1 to 4
Outputs:
- peak_stats: float32 [2, 524288], P(None, 'gauss')
- clones: float32 [61, 524288], P(None, 'gauss')
- clone_total: int32 [], replicated
Inputs may be any that keep to these rules, and one draw needn't show every extreme that they name: `clone_mask`: in every draw some shard of 16384 consecutive Gaussians has all of them marked.
All inputs are finite; a program needn't handle non-finite values. No bound on the sum of `visible` on one device may be relied on, other than what follows from the above.
Results may differ from a plain program's by a relative error of at most 0.0003.
Values sent between devices are 32-bit elements; how exact they have to be, the bound alone decides.
No kernel may reach another device: no remote copies, remote signals or barrier semaphores. Data moves between devices by JAX's collectives and lax.ppermute only.
A program may use at most 128 MiB of HBM per device.

v0:
```python
import jax
import jax.numpy as jnp
from jax import lax
from jax.sharding import PartitionSpec as P

G_DEV = 16384


def copy_for_each(x, axis):
    count = lax.axis_size(axis)
    return lax.all_to_all(jnp.broadcast_to(x[None], (count, *x.shape)), axis, 0, 0, tiled=True)


def of_everyone(x, axis):
    return copy_for_each(x, axis).max(axis=0)


def together(arrays, axis):
    vector, at, done = (jnp.concatenate([a.reshape(-1) for a in arrays]), 0, [])
    running = of_everyone(vector, axis)
    for a in arrays:
        done.append(running[at : at + a.size].reshape(a.shape))
        at += a.size
    return tuple(done)


def folded_in_pairs(pieces, combine):
    while len(jax.tree.leaves(pieces)[0]) > 1:
        pieces = jax.vmap(combine)(*(pieces[side::2] for side in (0, 1)))
    return pieces[0]


def prefix(x, axis, combine, identity):
    count, mine = (lax.axis_size(axis), lax.axis_index(axis))
    passed = jnp.arange(count) < mine

    def kept(part, zero, own):
        part = jnp.where(
            passed.reshape(-1, *(1 for _ in own.shape)), part, jnp.asarray(zero, own.dtype)
        )
        return part

    pieces = copy_for_each(x, axis)
    return folded_in_pairs(kept(pieces, identity, x), combine)


def of_everyone_2(x, axis):
    everything = copy_for_each(x, axis)
    return jnp.sum(everything, axis=0)


def quat_factor(scales, quats):
    inv = 1.0 / jnp.sqrt(jnp.sum(quats * quats, axis=0) + 0.25)
    w, x, y, z = (quats[0] * inv, quats[1] * inv, quats[2] * inv, quats[3] * inv)
    rq = [
        [1 - 2 * (y * y + z * z), 2 * (x * y - w * z), 2 * (x * z + w * y)],
        [2 * (x * y + w * z), 1 - 2 * (x * x + z * z), 2 * (y * z - w * x)],
        [2 * (x * z - w * y), 2 * (y * z + w * x), 1 - 2 * (x * x + y * y)],
    ]
    return [[rq[i][j] * scales[j] for j in range(3)] for i in range(3)]


def view_stats(means, factor, grad, seen, rot, trans, focal_v):
    point = [
        rot[i, 0] * means[0] + rot[i, 1] * means[1] + rot[i, 2] * means[2] + trans[i]
        for i in range(3)
    ]
    depth = jnp.maximum(point[2], 1.0)
    j00 = focal_v / depth
    j02 = -focal_v * point[0] / (depth * depth)
    j12 = -focal_v * point[1] / (depth * depth)
    first = [j00 * rot[0, j] + j02 * rot[2, j] for j in range(3)]
    second = [j00 * rot[1, j] + j12 * rot[2, j] for j in range(3)]
    prow = [sum((first[j] * factor[j][k] for j in range(3))) for k in range(3)]
    qrow = [sum((second[j] * factor[j][k] for j in range(3))) for k in range(3)]
    a_val = prow[0] ** 2 + prow[1] ** 2 + prow[2] ** 2 + 0.3
    c_val = qrow[0] ** 2 + qrow[1] ** 2 + qrow[2] ** 2 + 0.3
    b_val = prow[0] * qrow[0] + prow[1] * qrow[1] + prow[2] * qrow[2]
    half = 0.5 * (a_val - c_val)
    lam = 0.5 * (a_val + c_val) + jnp.sqrt(half * half + b_val * b_val + 0.01)
    seenf = seen.astype(jnp.float32)
    radius = 3.0 * jnp.sqrt(lam) * seenf
    gnorm = jnp.sqrt(grad[0] * grad[0] + grad[1] * grad[1]) * seenf
    return (gnorm, radius)


def add_ints(earlier, later):
    return earlier + later


def body(means, scales, quats, attrs, grad_screen, visible, clone_mask, rotation, shift, focal):
    factor = quat_factor(scales, quats)
    gmax = jnp.zeros(means.shape[1], jnp.float32)
    rmax = jnp.zeros(means.shape[1], jnp.float32)
    for v in range(grad_screen.shape[0]):
        gnorm, radius = view_stats(
            means, factor, grad_screen[v], visible[v], rotation[v], shift[v], focal[v]
        )
        gmax = jnp.maximum(gmax, gnorm)
        rmax = jnp.maximum(rmax, radius)
    gmax, rmax = together((gmax, rmax), "view")
    peak = jnp.stack([gmax, rmax])
    rows = jnp.concatenate([means, scales, quats, attrs, peak], axis=0)
    feat_rows = rows.shape[0]
    shards = lax.axis_size("gauss")
    cap_blk = G_DEV // 128
    count = jnp.sum(clone_mask)
    blocks = (count + 127) // 128
    offset = prefix(blocks, "gauss", add_ints, jnp.int32(0))
    summed = of_everyone_2(count.astype(jnp.float32), "gauss")
    total = summed.astype(jnp.int32)
    rank = jnp.cumsum(clone_mask) - 1
    where_to = jnp.where(clone_mask == 1, rank, cap_blk * 128)
    packed = (
        jnp.zeros((feat_rows, cap_blk * 128), jnp.float32).at[:, where_to].set(rows, mode="drop")
    )
    packed = packed.reshape(feat_rows, cap_blk, 128)
    per = (cap_blk + shards - 1) // shards
    target = jnp.arange(shards, dtype=jnp.int32)[:, None]
    within = jnp.arange(per, dtype=jnp.int32)[None, :]
    local_blk = (target - offset) % shards + within * shards
    valid = local_blk < blocks
    picked = jnp.minimum(local_blk, cap_blk - 1).reshape(-1)
    outgoing = packed[:, picked, :] * valid.reshape(1, -1, 1).astype(jnp.float32)
    outgoing = outgoing.reshape(feat_rows, shards, per, 128)
    slot_ids = (
        jnp.where(valid, (offset + local_blk) // shards, cap_blk)
        .astype(jnp.int32)
        .reshape(1, shards, per)
    )
    width = 128 // lax.axis_size("view")
    start = lax.axis_index("view") * width
    portion = lax.dynamic_slice_in_dim(outgoing, start, width, 3)
    arrived, slots_in = (
        lax.all_to_all(portion, "gauss", split_axis=1, concat_axis=1, tiled=True),
        lax.all_to_all(slot_ids, "gauss", split_axis=1, concat_axis=1, tiled=True),
    )
    arrived = arrived.reshape(feat_rows, shards * per, width)
    partial_place = (
        jnp.zeros((feat_rows, cap_blk, width), jnp.float32)
        .at[:, slots_in.reshape(-1)]
        .set(arrived, mode="drop")
    )
    placed = lax.all_gather(partial_place, "view", axis=2, tiled=True)
    clones = placed.reshape(feat_rows, cap_blk * 128)
    return (peak, clones, total)


def solution(mesh):
    return jax.shard_map(
        body,
        mesh=mesh,
        in_specs=(
            P(None, "gauss"),
            P(None, "gauss"),
            P(None, "gauss"),
            P(None, "gauss"),
            P("view", None, "gauss"),
            P("view", "gauss"),
            P("gauss"),
            P("view", None, None),
            P("view", None),
            P("view"),
        ),
        out_specs=(P(None, "gauss"), P(None, "gauss"), P()),
        check_vma=False,
    )
```

profile of v0, /device:TPU:1, one launch (start us, length us, event | category | flops | bytes accessed | tf_op | source)
XLA Modules:
  0.0 326.7 jit_solution(10295088173397887772)
XLA Ops:
  8.9 2.1 compare_select_fusion
  12.2 12.0 %all-to-all-start.1 = ((s32[32,1,1]{2,1,0:T(1,128)}), s32[32,1,1]{2,1,0:T(1,128)S(1)}, u32[]{:S(2)}, u32[]{:S(2)}) async-start(s32[32,1,1]{2,1,0:T(1,128)} %broadcast_in_dim.45), calls=%async_computation.1 | async-start | bytes 32768 | tf_op jit(solution)/shard_map/all_to_all | solution.py:11
  24.2 2.4 fusion.6
  29.9 1.8 fusion.11
  33.8 7.2 %multiply_add_fusion.23 = (f32[1,16384]{1,0:T(1,128)S(1)}, f32[1,16384]{1,0:T(1,128)S(1)}, f32[1,16384]{1,0:T(1,128)S(1)}, f32[1,16384]{1,0:T(1,128)S(1)}) fusion(f32[]{:T(128)} %bitcast.13, f32[]{:T(128)} %bitcast.9, f32[]{:T(128)} %bitcast.16, f32[3,16384]{1,0:T(4,128)} %param.10, f32[]{:T(128)} %bitcast.15, f32[]{:T(128)} %bitcast.14, f32[]{:T(128)S(6)} %neg.16, ...), kind=kLoop, calls=%fused_computation.35 | loop fusion | flops 327680 | bytes 458792 | tf_op jit(solution)/shard_map/add | solution.py:72
  41.1 7.3 %multiply_add_fusion.22 = (f32[1,16384]{1,0:T(1,128)S(1)}, f32[1,16384]{1,0:T(1,128)S(1)}, f32[1,16384]{1,0:T(1,128)S(1)}, f32[1,16384]{1,0:T(1,128)S(1)}) fusion(f32[1,16384]{1,0:T(1,128)S(1)} %get-tuple-element.22, f32[1,16384]{1,0:T(1,128)S(1)} %get-tuple-element.23, f32[]{:T(128)} %bitcast.14, f32[]{:T(128)} %bitcast.10, f32[]{:T(128)} %bitcast.11, ...), kind=kLoop, calls=%fused_computation.34 | loop fusion | flops 294912 | bytes 655400 | tf_op jit(solution)/shard_map/add | solution.py:72
  48.3 2.5 multiply_add_fusion.19
  52.2 7.4 %multiply_add_fusion.17 = (f32[1,16384]{1,0:T(1,128)S(1)}, f32[1,16384]{1,0:T(1,128)S(1)}, f32[1,16384]{1,0:T(1,128)S(1)}, f32[1,16384]{1,0:T(1,128)S(1)}) fusion(f32[]{:T(128)} %bitcast.39, f32[]{:T(128)} %bitcast.35, f32[]{:T(128)} %bitcast.42, f32[3,16384]{1,0:T(4,128)} %param.10, f32[]{:T(128)} %bitcast.41, f32[]{:T(128)} %bitcast.40, f32[]{:T(128)S(6)} %neg.17, ...), kind=kLoop, calls=%fused_computation.29 | loop fusion | flops 327680 | bytes 458792 | tf_op jit(solution)/shard_map/add | solution.py:72
  59.6 7.2 %multiply_add_fusion.16 = (f32[1,16384]{1,0:T(1,128)S(1)}, f32[1,16384]{1,0:T(1,128)S(1)}, f32[1,16384]{1,0:T(1,128)S(1)}, f32[1,16384]{1,0:T(1,128)S(1)}) fusion(f32[1,16384]{1,0:T(1,128)S(1)} %get-tuple-element.28, f32[1,16384]{1,0:T(1,128)S(1)} %get-tuple-element.29, f32[]{:T(128)} %bitcast.40, f32[]{:T(128)} %bitcast.36, f32[]{:T(128)} %bitcast.37, ...), kind=kLoop, calls=%fused_computation.28 | loop fusion | flops 294912 | bytes 655400 | tf_op jit(solution)/shard_map/add | solution.py:72
  66.8 2.5 multiply_add_fusion.13
  70.7 7.4 %multiply_add_fusion.11 = (f32[1,16384]{1,0:T(1,128)S(1)}, f32[1,16384]{1,0:T(1,128)S(1)}, f32[1,16384]{1,0:T(1,128)S(1)}, f32[1,16384]{1,0:T(1,128)S(1)}) fusion(f32[]{:T(128)} %bitcast.58, f32[]{:T(128)} %bitcast.54, f32[]{:T(128)} %bitcast.61, f32[3,16384]{1,0:T(4,128)} %param.10, f32[]{:T(128)} %bitcast.60, f32[]{:T(128)} %bitcast.59, f32[]{:T(128)S(6)} %neg.18, ...), kind=kLoop, calls=%fused_computation.23 | loop fusion | flops 327680 | bytes 458792 | tf_op jit(solution)/shard_map/add | solution.py:72
  78.1 7.4 %multiply_add_fusion.10 = (f32[1,16384]{1,0:T(1,128)S(1)}, f32[1,16384]{1,0:T(1,128)S(1)}, f32[1,16384]{1,0:T(1,128)S(1)}, f32[1,16384]{1,0:T(1,128)S(1)}) fusion(f32[1,16384]{1,0:T(1,128)S(1)} %get-tuple-element.34, f32[1,16384]{1,0:T(1,128)S(1)} %get-tuple-element.35, f32[]{:T(128)} %bitcast.59, f32[]{:T(128)} %bitcast.55, f32[]{:T(128)} %bitcast.56, ...), kind=kLoop, calls=%fused_computation.22 | loop fusion | flops 294912 | bytes 655400 | tf_op jit(solution)/shard_map/add | solution.py:72
  85.4 2.6 multiply_add_fusion.7
  89.4 7.4 %multiply_add_fusion.5 = (f32[1,16384]{1,0:T(1,128)S(1)}, f32[1,16384]{1,0:T(1,128)S(1)}, f32[1,16384]{1,0:T(1,128)S(1)}, f32[1,16384]{1,0:T(1,128)S(1)}) fusion(f32[]{:T(128)} %bitcast.77, f32[]{:T(128)} %bitcast.73, f32[]{:T(128)} %bitcast.80, f32[3,16384]{1,0:T(4,128)} %param.10, f32[]{:T(128)} %bitcast.79, f32[]{:T(128)} %bitcast.78, f32[]{:T(128)S(6)} %neg.19, ...), kind=kLoop, calls=%fused_computation.17 | loop fusion | flops 327680 | bytes 458792 | tf_op jit(solution)/shard_map/add | solution.py:72
  96.8 7.4 %multiply_add_fusion.4 = (f32[1,16384]{1,0:T(1,128)S(1)}, f32[1,16384]{1,0:T(1,128)S(1)}, f32[1,16384]{1,0:T(1,128)S(1)}, f32[1,16384]{1,0:T(1,128)S(1)}) fusion(f32[1,16384]{1,0:T(1,128)S(1)} %get-tuple-element.40, f32[1,16384]{1,0:T(1,128)S(1)} %get-tuple-element.41, f32[]{:T(128)} %bitcast.78, f32[]{:T(128)} %bitcast.74, f32[]{:T(128)} %bitcast.75, ...), kind=kLoop, calls=%fused_computation.16 | loop fusion | flops 294912 | bytes 655400 | tf_op jit(solution)/shard_map/add | solution.py:72
  104.2 2.6 multiply_add_fusion.1
  110.2 1.8 multiply_maximum_fusion
  113.5 5.3 %all-to-all-start = ((f32[8,1,32768]{2,1,0:T(1,128)}), f32[8,1,32768]{2,1,0:T(1,128)S(1)}, u32[]{:S(2)}, u32[]{:S(2)}) async-start(f32[8,1,32768]{2,1,0:T(1,128)} %broadcast_in_dim.24), calls=%async_computation | async-start | bytes 2097152 | tf_op jit(solution)/shard_map/all_to_all | solution.py:11
  125.2 8.5 %all-to-all-done = f32[8,1,32768]{2,1,0:T(1,128)S(1)} async-done(((f32[8,1,32768]{2,1,0:T(1,128)}), f32[8,1,32768]{2,1,0:T(1,128)S(1)}, u32[]{:S(2)}, u32[]{:S(2)}) %all-to-all-start) | async-done | bytes 1048608 | tf_op jit(solution)/shard_map/all_to_all | solution.py:11
  133.7 9.7 %all-to-all-start.2 = ((s32[1,32,4]{2,0,1:T(1,128)}), s32[1,32,4]{2,0,1:T(1,128)S(1)}, u32[]{:S(2)}, u32[]{:S(2)}) async-start(s32[1,32,4]{2,0,1:T(1,128)} %compare_select_fusion.1), calls=%async_computation.2 | async-start | bytes 32768 | tf_op jit(solution)/shard_map/all_to_all | solution.py:136
  144.2 21.5 %concatenate.8 = f32[61,16384]{1,0:T(8,128)} concatenate(f32[3,16384]{1,0:T(4,128)S(1)} %copy-done.1, f32[3,16384]{1,0:T(4,128)S(1)} %copy-done.3, f32[4,16384]{1,0:T(4,128)S(1)} %copy-done.2, f32[49,16384]{1,0:T(8,128)} %param.13, f32[1,16384]{1,0:T(1,128)S(1)} %bitcast.129, f32[1,16384]{1,0:T(1,128)S(1)} %bitcast.131), dimensions={0} | concatenate | bytes 7995392 | tf_op jit(solution)/shard_map/concatenate | solution.py:103
  165.8 6.9 %copy.40 = f32[16384,61]{1,0:T(8,128)} copy(f32[16384,61]{0,1:T(8,128)} %bitcast.126) | data formatting | bytes 7995392 | tf_op jit(solution)/shard_map/concatenate | solution.py:103
  172.7 44.3 %scatter_custom_fusion = f32[61,16384]{0,1:T(8,128)} fusion(s32[16384]{0:T(1024)} %get-tuple-element.78, f32[16384,61]{1,0:T(8,128)} %copy.40, f32[]{:T(128)} %constant.32.clone.1), kind=kCustom, calls=%fused_computation.3 | custom fusion | bytes 3998208 | tf_op jit(solution)/shard_map/scatter | solution.py:115
  217.0 7.7 %gather_fusion = f32[128,61,128]{1,2,0:T(8,128)} fusion(f32[61,128,128]{0,2,1:T(8,128)} %bitcast.125, s32[1024]{0:T(1024)S(1)} %pad_clamp_fusion), kind=kCustom, calls=%fused_computation | custom fusion | bytes 7995904 | tf_op jit(solution)/shard_map/gather | solution.py:124
  226.2 2.3 reshape.640
  228.5 9.1 %all-to-all-start.3 = ((f32[32,1,3904]{2,1,0:T(1,128)}), f32[32,1,3904]{2,1,0:T(1,128)S(1)}, u32[]{:S(2)}, u32[]{:S(2)}) async-start(f32[32,1,3904]{2,1,0:T(1,128)} %reshape.640), calls=%async_computation.3 | async-start | bytes 1015808 | tf_op jit(solution)/shard_map/all_to_all | solution.py:135
  238.9 11.3 %all-to-all-done.3 = f32[32,1,3904]{2,1,0:T(1,128)S(1)} async-done(((f32[32,1,3904]{2,1,0:T(1,128)}), f32[32,1,3904]{2,1,0:T(1,128)S(1)}, u32[]{:S(2)}, u32[]{:S(2)}) %all-to-all-start.3) | async-done | bytes 499744 | tf_op jit(solution)/shard_map/all_to_all | solution.py:135
  250.8 1.8 reduce.9
  254.2 4.5 %scatter_fusion = f32[61,128,16]{0,2,1:T(8,128)S(1)} fusion(f32[61,128,16]{0,2,1:T(8,128)S(1)} %broadcast_in_dim.44, s32[128]{0:T(128)S(1)} %fusion.4, f32[128,61,16]{1,2,0:T(8,128)S(1)} %bitcast.124), kind=kCustom, calls=%fused_computation.2 | custom fusion | bytes 1499648 | tf_op jit(solution)/shard_map/scatter | solution.py:142
  260.3 16.9 %all_to_all.31 = f32[32,1,1]{2,1,0:T(1,128)S(1)} all-to-all(f32[32,1,1]{2,1,0:T(1,128)S(1)} %broadcast_in_dim.51), channel_id=1, replica_groups=mesh['view'=8,'gauss'=32] {'gauss'}, dimensions={0} | all-to-all | bytes 256 | tf_op jit(solution)/shard_map/all_to_all | solution.py:11
  279.3 32.5 %all-gather.2.cloned.1.call-done = f32[61,128,128]{0,2,1:T(8,128)} async-done(((f32[61,128,16]{0,2,1:T(8,128)}), f32[61,128,128]{0,2,1:T(8,128)}) %all-gather.2.cloned.1.call-update) | async-done | bytes 3997712 | tf_op jit(solution)/shard_map/all_gather | solution.py:144
  311.8 6.8 %copy.42 = f32[61,16384]{1,0:T(8,128)} copy(f32[61,16384]{0,1:T(8,128)} %bitcast.127) | data formatting | bytes 7995392
  (74 shorter events, 27.1 us)
Async XLA Ops:
  7.2 101.4 %copy-start.3 = (f32[3,16384]{1,0:T(4,128)S(1)}, f32[3,16384]{1,0:T(4,128)}, u32[]{:S(2)}) copy-start(f32[3,16384]{1,0:T(4,128)} %param.11) | copy-start | bytes 589828
  7.2 102.1 %copy-start.4 = (f32[4,2,16384]{2,1,0:T(2,128)S(1)}, f32[4,2,16384]{2,1,0:T(2,128)}, u32[]{:S(2)}) copy-start(f32[4,2,16384]{2,1,0:T(2,128)} %param.14) | copy-start | bytes 1572868
  12.2 99.8 %all-to-all-start.1 = ((s32[32,1,1]{2,1,0:T(1,128)}), s32[32,1,1]{2,1,0:T(1,128)S(1)}, u32[]{:S(2)}, u32[]{:S(2)}) async-start(s32[32,1,1]{2,1,0:T(1,128)} %broadcast_in_dim.45), calls=%async_computation.1 | async-start | bytes 32768 | tf_op jit(solution)/shard_map/all_to_all | solution.py:11
  24.2 120.0 %copy-start.1 = (f32[3,16384]{1,0:T(4,128)S(1)}, f32[3,16384]{1,0:T(4,128)}, u32[]{:S(2)}) copy-start(f32[3,16384]{1,0:T(4,128)} %param.10) | copy-start | bytes 589828
  24.2 120.0 %copy-start.2 = (f32[4,16384]{1,0:T(4,128)S(1)}, f32[4,16384]{1,0:T(4,128)}, u32[]{:S(2)}) copy-start(f32[4,16384]{1,0:T(4,128)} %param.12) | copy-start | bytes 786436
  113.5 20.2 %all-to-all-start = ((f32[8,1,32768]{2,1,0:T(1,128)}), f32[8,1,32768]{2,1,0:T(1,128)S(1)}, u32[]{:S(2)}, u32[]{:S(2)}) async-start(f32[8,1,32768]{2,1,0:T(1,128)} %broadcast_in_dim.24), calls=%async_computation | async-start | bytes 2097152 | tf_op jit(solution)/shard_map/all_to_all | solution.py:11
  133.7 94.8 %all-to-all-start.2 = ((s32[1,32,4]{2,0,1:T(1,128)}), s32[1,32,4]{2,0,1:T(1,128)S(1)}, u32[]{:S(2)}, u32[]{:S(2)}) async-start(s32[1,32,4]{2,0,1:T(1,128)} %compare_select_fusion.1), calls=%async_computation.2 | async-start | bytes 32768 | tf_op jit(solution)/shard_map/all_to_all | solution.py:136
  228.5 21.8 %all-to-all-start.3 = ((f32[32,1,3904]{2,1,0:T(1,128)}), f32[32,1,3904]{2,1,0:T(1,128)S(1)}, u32[]{:S(2)}, u32[]{:S(2)}) async-start(f32[32,1,3904]{2,1,0:T(1,128)} %reshape.640), calls=%async_computation.3 | async-start | bytes 1015808 | tf_op jit(solution)/shard_map/all_to_all | solution.py:135
  237.6 74.3 %all-gather.2.cloned.1.call-start = ((), (), s32[]{:S(2)}) async-start(), calls=%async_computation.5 | async-start | bytes 9437184 | tf_op jit(solution)/shard_map/all_gather | solution.py:144
  258.8 1.0 copy-start
Sparse Core Ops, SparseCore 0:
  259.9 51.9 all-gather.1
where the time goes:
time: 329 us; the launch traced here: 327 us
  local copies, waits for them, and re-layouts  113 us (34%)
  other arithmetic  87.1 us (26%)
  waiting for transfers between devices  52.4 us (16%)
  starting transfers between devices  36.1 us (11%)
  between operations  21.3 us (6%)
  blocking collectives  16.9 us (5%)
    add x8, other arithmetic, view_stats(): first = [j00 * rot[0, j] + j02 * rot[2, j] for j in range(3)]  58.6 us
    scatter x1, local copies, waits for them, and re-layouts, body(): jnp.zeros((feat_rows, cap_blk * 128), jnp.float32).at[:, where_to]  44.3 us
    all_gather x1, waiting for transfers between devices, body(): placed = lax.all_gather(partial_place, 'view', axis=2, tiled=True)  32.5 us
    concatenate x2, local copies, waits for them, and re-layouts, body(): rows = jnp.concatenate([means, scales, quats, attrs, peak], axis=0)  28.5 us
    all_to_all x2, starting transfers between devices, copy_for_each(): lax.all_to_all(jnp.broadcast_to(x[None], (count, *x.shape)), axis, 0, 0,...  17.3 us
    all_to_all x1, blocking collectives, copy_for_each(): lax.all_to_all(jnp.broadcast_to(x[None], (count, *x.shape)), axis, 0, 0,...  16.9 us
    unnamed x15, local copies, waits for them, and re-layouts  11.7 us
    all_to_all x1, waiting for transfers between devices, body(): lax.all_to_all(portion, 'gauss', split_axis=1, concat_axis=1, tiled=True)  11.3 us
  transfers between devices with their start and end apart: 5, of which 3 were waited for; matrix products, arithmetic and copies ran while one was open for 54% of the time, Pallas kernels for 0%

commit v1 on v0

--- a/solution.py
+++ b/solution.py
@@ -132,7 +132,12 @@
     start = lax.axis_index("view") * width
     portion = lax.dynamic_slice_in_dim(outgoing, start, width, 3)
     arrived, slots_in = (
-        lax.all_to_all(portion, "gauss", split_axis=1, concat_axis=1, tiled=True),
+        jnp.concatenate(
+            lax.all_to_all(
+                jnp.stack(jnp.split(portion, lax.axis_size("gauss"), axis=1)), "gauss", 0, 0
+            ),
+            axis=1,
+        ),
         lax.all_to_all(slot_ids, "gauss", split_axis=1, concat_axis=1, tiled=True),
     )
     arrived = arrived.reshape(feat_rows, shards * per, width)

time: 329 us -> 330 us (level)
    unnamed x15 -> x46, local copies, waits for them, and re-layouts: 11.7 us -> 11.8 us
where the time goes in v1:
time: 330 us; the launch traced here: 327 us
  local copies, waits for them, and re-layouts  113 us (34%)
  other arithmetic  87.2 us (26%)
  waiting for transfers between devices  52.4 us (16%)
  starting transfers between devices  36.1 us (11%)
  between operations  21.5 us (7%)
  blocking collectives  16.9 us (5%)
    add x8, other arithmetic, view_stats(): first = [j00 * rot[0, j] + j02 * rot[2, j] for j in range(3)]  58.6 us
    scatter x1, local copies, waits for them, and re-layouts, body(): jnp.zeros((feat_rows, cap_blk * 128), jnp.float32).at[:, where_to]  44.3 us
    all_gather x1, waiting for transfers between devices, body(): placed = lax.all_gather(partial_place, 'view', axis=2, tiled=True)  32.5 us
    concatenate x2, local copies, waits for them, and re-layouts, body(): rows = jnp.concatenate([means, scales, quats, attrs, peak], axis=0)  28.5 us
    all_to_all x2, starting transfers between devices, copy_for_each(): lax.all_to_all(jnp.broadcast_to(x[None], (count, *x.shape)), axis, 0, 0,...  17.3 us
    all_to_all x1, blocking collectives, copy_for_each(): lax.all_to_all(jnp.broadcast_to(x[None], (count, *x.shape)), axis, 0, 0,...  16.9 us
    unnamed x46, local copies, waits for them, and re-layouts  11.8 us
    all_to_all x1, waiting for transfers between devices, body(): lax.all_to_all(jnp.stack(jnp.split(portion, lax.axis_size('gauss'), axis=...  11.3 us
  transfers between devices with their start and end apart: 5, of which 3 were waited for; matrix products, arithmetic and copies ran while one was open for 54% of the time, Pallas kernels for 0%

profile of v1, /device:TPU:1, one launch (start us, length us, event | category | flops | bytes accessed | tf_op | source)
XLA Modules:
  0.0 327.1 jit_solution(16063473621375712980)
XLA Ops:
  8.9 2.1 compare_select_fusion
  12.2 12.0 %all-to-all-start.1 = ((s32[32,1,1]{2,1,0:T(1,128)}), s32[32,1,1]{2,1,0:T(1,128)S(1)}, u32[]{:S(2)}, u32[]{:S(2)}) async-start(s32[32,1,1]{2,1,0:T(1,128)} %broadcast_in_dim.45), calls=%async_computation.1 | async-start | bytes 32768 | tf_op jit(solution)/shard_map/all_to_all | solution.py:11
  24.2 2.4 fusion.6
  29.9 1.8 fusion.11
  33.8 7.2 %multiply_add_fusion.23 = (f32[1,16384]{1,0:T(1,128)S(1)}, f32[1,16384]{1,0:T(1,128)S(1)}, f32[1,16384]{1,0:T(1,128)S(1)}, f32[1,16384]{1,0:T(1,128)S(1)}) fusion(f32[]{:T(128)} %bitcast.13, f32[]{:T(128)} %bitcast.9, f32[]{:T(128)} %bitcast.16, f32[3,16384]{1,0:T(4,128)} %param.10, f32[]{:T(128)} %bitcast.15, f32[]{:T(128)} %bitcast.14, f32[]{:T(128)S(6)} %neg.16, ...), kind=kLoop, calls=%fused_computation.67 | loop fusion | flops 327680 | bytes 458792 | tf_op jit(solution)/shard_map/add | solution.py:72
  41.1 7.3 %multiply_add_fusion.22 = (f32[1,16384]{1,0:T(1,128)S(1)}, f32[1,16384]{1,0:T(1,128)S(1)}, f32[1,16384]{1,0:T(1,128)S(1)}, f32[1,16384]{1,0:T(1,128)S(1)}) fusion(f32[1,16384]{1,0:T(1,128)S(1)} %get-tuple-element.22, f32[1,16384]{1,0:T(1,128)S(1)} %get-tuple-element.23, f32[]{:T(128)} %bitcast.14, f32[]{:T(128)} %bitcast.10, f32[]{:T(128)} %bitcast.11, ...), kind=kLoop, calls=%fused_computation.66 | loop fusion | flops 294912 | bytes 655400 | tf_op jit(solution)/shard_map/add | solution.py:72
  48.3 2.5 multiply_add_fusion.19
  52.2 7.4 %multiply_add_fusion.17 = (f32[1,16384]{1,0:T(1,128)S(1)}, f32[1,16384]{1,0:T(1,128)S(1)}, f32[1,16384]{1,0:T(1,128)S(1)}, f32[1,16384]{1,0:T(1,128)S(1)}) fusion(f32[]{:T(128)} %bitcast.39, f32[]{:T(128)} %bitcast.35, f32[]{:T(128)} %bitcast.42, f32[3,16384]{1,0:T(4,128)} %param.10, f32[]{:T(128)} %bitcast.41, f32[]{:T(128)} %bitcast.40, f32[]{:T(128)S(6)} %neg.17, ...), kind=kLoop, calls=%fused_computation.61 | loop fusion | flops 327680 | bytes 458792 | tf_op jit(solution)/shard_map/add | solution.py:72
  59.6 7.2 %multiply_add_fusion.16 = (f32[1,16384]{1,0:T(1,128)S(1)}, f32[1,16384]{1,0:T(1,128)S(1)}, f32[1,16384]{1,0:T(1,128)S(1)}, f32[1,16384]{1,0:T(1,128)S(1)}) fusion(f32[1,16384]{1,0:T(1,128)S(1)} %get-tuple-element.28, f32[1,16384]{1,0:T(1,128)S(1)} %get-tuple-element.29, f32[]{:T(128)} %bitcast.40, f32[]{:T(128)} %bitcast.36, f32[]{:T(128)} %bitcast.37, ...), kind=kLoop, calls=%fused_computation.60 | loop fusion | flops 294912 | bytes 655400 | tf_op jit(solution)/shard_map/add | solution.py:72
  66.8 2.5 multiply_add_fusion.13
  70.7 7.4 %multiply_add_fusion.11 = (f32[1,16384]{1,0:T(1,128)S(1)}, f32[1,16384]{1,0:T(1,128)S(1)}, f32[1,16384]{1,0:T(1,128)S(1)}, f32[1,16384]{1,0:T(1,128)S(1)}) fusion(f32[]{:T(128)} %bitcast.58, f32[]{:T(128)} %bitcast.54, f32[]{:T(128)} %bitcast.61, f32[3,16384]{1,0:T(4,128)} %param.10, f32[]{:T(128)} %bitcast.60, f32[]{:T(128)} %bitcast.59, f32[]{:T(128)S(6)} %neg.18, ...), kind=kLoop, calls=%fused_computation.55 | loop fusion | flops 327680 | bytes 458792 | tf_op jit(solution)/shard_map/add | solution.py:72
  78.1 7.4 %multiply_add_fusion.10 = (f32[1,16384]{1,0:T(1,128)S(1)}, f32[1,16384]{1,0:T(1,128)S(1)}, f32[1,16384]{1,0:T(1,128)S(1)}, f32[1,16384]{1,0:T(1,128)S(1)}) fusion(f32[1,16384]{1,0:T(1,128)S(1)} %get-tuple-element.34, f32[1,16384]{1,0:T(1,128)S(1)} %get-tuple-element.35, f32[]{:T(128)} %bitcast.59, f32[]{:T(128)} %bitcast.55, f32[]{:T(128)} %bitcast.56, ...), kind=kLoop, calls=%fused_computation.54 | loop fusion | flops 294912 | bytes 655400 | tf_op jit(solution)/shard_map/add | solution.py:72
  85.5 2.6 multiply_add_fusion.7
  89.5 7.4 %multiply_add_fusion.5 = (f32[1,16384]{1,0:T(1,128)S(1)}, f32[1,16384]{1,0:T(1,128)S(1)}, f32[1,16384]{1,0:T(1,128)S(1)}, f32[1,16384]{1,0:T(1,128)S(1)}) fusion(f32[]{:T(128)} %bitcast.77, f32[]{:T(128)} %bitcast.73, f32[]{:T(128)} %bitcast.80, f32[3,16384]{1,0:T(4,128)} %param.10, f32[]{:T(128)} %bitcast.79, f32[]{:T(128)} %bitcast.78, f32[]{:T(128)S(6)} %neg.19, ...), kind=kLoop, calls=%fused_computation.49 | loop fusion | flops 327680 | bytes 458792 | tf_op jit(solution)/shard_map/add | solution.py:72
  96.8 7.4 %multiply_add_fusion.4 = (f32[1,16384]{1,0:T(1,128)S(1)}, f32[1,16384]{1,0:T(1,128)S(1)}, f32[1,16384]{1,0:T(1,128)S(1)}, f32[1,16384]{1,0:T(1,128)S(1)}) fusion(f32[1,16384]{1,0:T(1,128)S(1)} %get-tuple-element.40, f32[1,16384]{1,0:T(1,128)S(1)} %get-tuple-element.41, f32[]{:T(128)} %bitcast.78, f32[]{:T(128)} %bitcast.74, f32[]{:T(128)} %bitcast.75, ...), kind=kLoop, calls=%fused_computation.48 | loop fusion | flops 294912 | bytes 655400 | tf_op jit(solution)/shard_map/add | solution.py:72
  104.2 2.6 multiply_add_fusion.1
  110.2 1.8 multiply_maximum_fusion
  113.5 5.3 %all-to-all-start = ((f32[8,1,32768]{2,1,0:T(1,128)}), f32[8,1,32768]{2,1,0:T(1,128)S(1)}, u32[]{:S(2)}, u32[]{:S(2)}) async-start(f32[8,1,32768]{2,1,0:T(1,128)} %broadcast_in_dim.24), calls=%async_computation | async-start | bytes 2097152 | tf_op jit(solution)/shard_map/all_to_all | solution.py:11
  125.2 8.5 %all-to-all-done = f32[8,1,32768]{2,1,0:T(1,128)S(1)} async-done(((f32[8,1,32768]{2,1,0:T(1,128)}), f32[8,1,32768]{2,1,0:T(1,128)S(1)}, u32[]{:S(2)}, u32[]{:S(2)}) %all-to-all-start) | async-done | bytes 1048608 | tf_op jit(solution)/shard_map/all_to_all | solution.py:11
  133.8 9.7 %all-to-all-start.2 = ((s32[1,32,4]{2,0,1:T(1,128)}), s32[1,32,4]{2,0,1:T(1,128)S(1)}, u32[]{:S(2)}, u32[]{:S(2)}) async-start(s32[1,32,4]{2,0,1:T(1,128)} %compare_select_fusion.1), calls=%async_computation.2 | async-start | bytes 32768 | tf_op jit(solution)/shard_map/all_to_all | solution.py:141
  144.3 21.5 %concatenate.8 = f32[61,16384]{1,0:T(8,128)} concatenate(f32[3,16384]{1,0:T(4,128)S(1)} %copy-done.1, f32[3,16384]{1,0:T(4,128)S(1)} %copy-done.3, f32[4,16384]{1,0:T(4,128)S(1)} %copy-done.2, f32[49,16384]{1,0:T(8,128)} %param.13, f32[1,16384]{1,0:T(1,128)S(1)} %bitcast.259, f32[1,16384]{1,0:T(1,128)S(1)} %bitcast.261), dimensions={0} | concatenate | bytes 7995392 | tf_op jit(solution)/shard_map/concatenate | solution.py:103
  165.8 6.9 %copy.102 = f32[16384,61]{1,0:T(8,128)} copy(f32[16384,61]{0,1:T(8,128)} %bitcast.255) | data formatting | bytes 7995392 | tf_op jit(solution)/shard_map/concatenate | solution.py:103
  172.7 44.3 %scatter_custom_fusion = f32[61,16384]{0,1:T(8,128)} fusion(s32[16384]{0:T(1024)} %get-tuple-element.78, f32[16384,61]{1,0:T(8,128)} %copy.102, f32[]{:T(128)} %constant.32.clone.1), kind=kCustom, calls=%fused_computation.3 | custom fusion | bytes 3998208 | tf_op jit(solution)/shard_map/scatter | solution.py:115
  217.1 7.7 %gather_fusion = f32[128,61,128]{1,2,0:T(8,128)} fusion(f32[61,128,128]{0,2,1:T(8,128)} %bitcast.254, s32[1024]{0:T(1024)S(1)} %pad_clamp_fusion), kind=kCustom, calls=%fused_computation | custom fusion | bytes 7995904 | tf_op jit(solution)/shard_map/gather | solution.py:124
  226.6 2.3 reshape.640
  229.0 9.1 %all-to-all-start.3 = ((f32[32,1,3904]{2,1,0:T(1,128)}), f32[32,1,3904]{2,1,0:T(1,128)S(1)}, u32[]{:S(2)}, u32[]{:S(2)}) async-start(f32[32,1,3904]{2,1,0:T(1,128)} %reshape.640), calls=%async_computation.3 | async-start | bytes 1015808 | tf_op jit(solution)/shard_map/all_to_all | solution.py:136
  239.4 11.3 %all-to-all-done.3 = f32[32,1,3904]{2,1,0:T(1,128)S(1)} async-done(((f32[32,1,3904]{2,1,0:T(1,128)}), f32[32,1,3904]{2,1,0:T(1,128)S(1)}, u32[]{:S(2)}, u32[]{:S(2)}) %all-to-all-start.3) | async-done | bytes 499744 | tf_op jit(solution)/shard_map/all_to_all | solution.py:136
  251.2 1.8 reduce.9
  254.7 4.5 %scatter_fusion = f32[61,128,16]{0,2,1:T(8,128)S(1)} fusion(f32[61,128,16]{0,2,1:T(8,128)S(1)} %broadcast_in_dim.44, s32[128]{0:T(128)S(1)} %fusion.4, f32[128,61,16]{1,2,0:T(8,128)S(1)} %bitcast.253), kind=kCustom, calls=%fused_computation.2 | custom fusion | bytes 1499648 | tf_op jit(solution)/shard_map/scatter | solution.py:147
  260.8 16.9 %all_to_all.31 = f32[32,1,1]{2,1,0:T(1,128)S(1)} all-to-all(f32[32,1,1]{2,1,0:T(1,128)S(1)} %broadcast_in_dim.51), channel_id=1, replica_groups=mesh['view'=8,'gauss'=32] {'gauss'}, dimensions={0} | all-to-all | bytes 256 | tf_op jit(solution)/shard_map/all_to_all | solution.py:11
  279.8 32.5 %all-gather.2.cloned.1.call-done = f32[61,128,128]{0,2,1:T(8,128)} async-done(((f32[61,128,16]{0,2,1:T(8,128)}), f32[61,128,128]{0,2,1:T(8,128)}) %all-gather.2.cloned.1.call-update) | async-done | bytes 3997712 | tf_op jit(solution)/shard_map/all_gather | solution.py:149
  312.3 6.8 %copy.104 = f32[61,16384]{1,0:T(8,128)} copy(f32[61,16384]{0,1:T(8,128)} %bitcast.256) | data formatting | bytes 7995392
  (106 shorter events, 27.3 us)
Async XLA Ops:
  7.2 101.4 %copy-start.3 = (f32[3,16384]{1,0:T(4,128)S(1)}, f32[3,16384]{1,0:T(4,128)}, u32[]{:S(2)}) copy-start(f32[3,16384]{1,0:T(4,128)} %param.11) | copy-start | bytes 589828
  7.2 102.2 %copy-start.4 = (f32[4,2,16384]{2,1,0:T(2,128)S(1)}, f32[4,2,16384]{2,1,0:T(2,128)}, u32[]{:S(2)}) copy-start(f32[4,2,16384]{2,1,0:T(2,128)} %param.14) | copy-start | bytes 1572868
  12.2 99.8 %all-to-all-start.1 = ((s32[32,1,1]{2,1,0:T(1,128)}), s32[32,1,1]{2,1,0:T(1,128)S(1)}, u32[]{:S(2)}, u32[]{:S(2)}) async-start(s32[32,1,1]{2,1,0:T(1,128)} %broadcast_in_dim.45), calls=%async_computation.1 | async-start | bytes 32768 | tf_op jit(solution)/shard_map/all_to_all | solution.py:11
  24.2 120.0 %copy-start.1 = (f32[3,16384]{1,0:T(4,128)S(1)}, f32[3,16384]{1,0:T(4,128)}, u32[]{:S(2)}) copy-start(f32[3,16384]{1,0:T(4,128)} %param.10) | copy-start | bytes 589828
  24.2 120.0 %copy-start.2 = (f32[4,16384]{1,0:T(4,128)S(1)}, f32[4,16384]{1,0:T(4,128)}, u32[]{:S(2)}) copy-start(f32[4,16384]{1,0:T(4,128)} %param.12) | copy-start | bytes 786436
  113.5 20.2 %all-to-all-start = ((f32[8,1,32768]{2,1,0:T(1,128)}), f32[8,1,32768]{2,1,0:T(1,128)S(1)}, u32[]{:S(2)}, u32[]{:S(2)}) async-start(f32[8,1,32768]{2,1,0:T(1,128)} %broadcast_in_dim.24), calls=%async_computation | async-start | bytes 2097152 | tf_op jit(solution)/shard_map/all_to_all | solution.py:11
  133.8 95.2 %all-to-all-start.2 = ((s32[1,32,4]{2,0,1:T(1,128)}), s32[1,32,4]{2,0,1:T(1,128)S(1)}, u32[]{:S(2)}, u32[]{:S(2)}) async-start(s32[1,32,4]{2,0,1:T(1,128)} %compare_select_fusion.1), calls=%async_computation.2 | async-start | bytes 32768 | tf_op jit(solution)/shard_map/all_to_all | solution.py:141
  229.0 21.8 %all-to-all-start.3 = ((f32[32,1,3904]{2,1,0:T(1,128)}), f32[32,1,3904]{2,1,0:T(1,128)S(1)}, u32[]{:S(2)}, u32[]{:S(2)}) async-start(f32[32,1,3904]{2,1,0:T(1,128)} %reshape.640), calls=%async_computation.3 | async-start | bytes 1015808 | tf_op jit(solution)/shard_map/all_to_all | solution.py:136
  238.0 74.3 %all-gather.2.cloned.1.call-start = ((), (), s32[]{:S(2)}) async-start(), calls=%async_computation.5 | async-start | bytes 9437184 | tf_op jit(solution)/shard_map/all_gather | solution.py:149
  259.2 1.0 copy-start
Sparse Core Ops, SparseCore 0:
  260.3 51.9 all-gather.1
